TPU v7x, 1024 devices: a whole 4x8x16 slice. The times are simulated.
1024 devices in a mesh: dom: 256 (over y, z, core), sub: 4 (over x).
Axes of the slice: x: 4, y: 8, z: 16, core: 2. Of those that a mesh axis runs over, the one named last changes fastest.
Arguments:
- dofs: float32 [9, 56, 16384], P(None, None, ('dom', 'sub')), may hold values from -6 to 6
- stiffness: float32 [3, 56, 56], replicated, may hold values from -0.75 to 0.75
- projection: float32 [4, 21, 56], replicated, may hold values from -0.75 to 0.75
- star: float32 [3, 9, 9, 16384], P(None, None, None, ('dom', 'sub')), may hold values from -1.25 to 1.25
- flux_minus: float32 [4, 9, 9, 16384], P(None, None, None, ('dom', 'sub')), may hold values from -1 to 1
- flux_plus: float32 [4, 9, 9, 16384], P(None, None, None, ('dom', 'sub')), may hold values from -1 to 1
- fault_flux: float32 [9, 9], replicated, may hold values from -2 to 2
- fault_faces: int32 [4, 16384], P(None, ('dom', 'sub')), may hold values 0 or 1
- levels: int32 [16384], P(('dom', 'sub')), may hold values from 0 to 1, as said below
- face_source: int32 [4, 16384], P(None, ('dom', 'sub')), may hold values from 0 to 111
- send_source: int32 [4096], P(('dom', 'sub')), may hold values from 0 to 63
Outputs:
- dofs_after: float32 [9, 56, 16384], P(None, None, ('dom', 'sub'))
Inputs may be any that keep to these rules, and one draw needn't show every extreme that they name: `levels`: on every device at most 8 of its 16 elements have level 0, and some device has exactly 8.
All inputs are finite; a program needn't handle non-finite values. No bound on the sum of `fault_faces` on one device may be relied on, other than what follows from the above.
Results may differ from a plain program's by a relative error of at most 0.0001.
Values sent between devices are 32-bit elements; how exact they have to be, the bound alone decides.
A program may use at most 64 MiB of HBM per device.

v0:
```python
import math

import jax
import jax.numpy as jnp
from jax import lax
from jax.sharding import PartitionSpec as P

ORDER = 6


fine_step = 0.75
exact_reference = lax.Precision.HIGHEST


def from_everyone(value, axis):
    copies = jnp.broadcast_to(value, (lax.axis_size(axis), *value.shape))
    return lax.all_to_all(copies, axis, split_axis=0, concat_axis=0, tiled=True)


def joined_along(blocks, dim):
    shape = list(blocks.shape[1:])
    shape[dim] *= blocks.shape[0]
    return jnp.moveaxis(blocks, 0, dim).reshape(shape)


def collect(value, axis, dim):
    blocks = from_everyone(value, axis)
    return joined_along(blocks, dim)


def padded(value, sides, width):
    for axis, dim in sides:
        count, length = (lax.axis_size(axis), value.shape[dim])
        up = [(i, (i + 1) % count) for i in range(count)]
        down = [(j, i) for i, j in up]
        last = lax.slice_in_dim(value, length - width, length, axis=dim)
        first = lax.slice_in_dim(value, 0, width, axis=dim)
        before = lax.ppermute(last, axis, up)
        after = lax.ppermute(first, axis, down)
        value = jnp.concatenate([before, value, after], axis=dim)
    return value


def taylor_weights(start_time, stop_time, term_count):
    return [
        (stop_time ** (term + 1) - start_time ** (term + 1)) / math.factorial(term + 1)
        for term in range(term_count)
    ]


def derivatives(state_now, stiffness, star_contribution):
    taylor_series = [state_now]
    for repeat in range(ORDER - 1):
        time_slopes = jnp.einsum(
            "dmn,wne->dwme", stiffness, taylor_series[-1], precision=exact_reference
        )
        taylor_series.append(
            jnp.einsum("usij,uifj->sfj", star_contribution, time_slopes, precision=exact_reference)
        )
    return jnp.stack(taylor_series)


def integrate(taylor_series, start_time, stop_time):
    quadrature_weights = jnp.array(
        taylor_weights(start_time, stop_time, taylor_series.shape[0]), jnp.float32
    )
    return jnp.einsum("h,hlui->lui", quadrature_weights, taylor_series, precision=exact_reference)


def face_values(field_state, projection):
    return jnp.einsum("bly,qyp->qlbp", projection, field_state, precision=exact_reference)


def advance(
    state_now,
    own_part,
    own_faces,
    beside,
    stiffness,
    projection,
    star_contribution,
    minus_part,
    coupling_part,
):
    incoming_flux = jnp.einsum(
        "dvwe,wne->dvne", star_contribution, own_part, precision=exact_reference
    )
    volume_term = jnp.einsum("utx,uytz->yxz", stiffness, incoming_flux, precision=exact_reference)
    flux_terms = jnp.einsum("fvwe,wjfe->vjfe", minus_part, own_faces, precision=exact_reference)
    flux_terms = flux_terms + jnp.einsum(
        "fvwe,wjfe->vjfe", coupling_part, beside, precision=exact_reference
    )
    surface_term = jnp.einsum("alz,qlad->qzd", projection, flux_terms, precision=exact_reference)
    return state_now + volume_term - surface_term


def exported(buffer):
    grouped = collect(buffer, "sub", 2)
    stack_count, face_width, slot_count = grouped.shape
    neighbours_all = padded(
        grouped.reshape(stack_count, face_width, 1, slot_count), (("dom", 2),), 1
    )
    return neighbours_all.reshape(stack_count, face_width, 3 * slot_count)


def per_device(
    dofs,
    stiffness,
    projection,
    star,
    flux_minus,
    flux_plus,
    fault_flux,
    fault_faces,
    levels,
    face_source,
    send_source,
):
    var_count = dofs.shape[0]
    elem_count = dofs.shape[2]
    face_width = var_count * projection.shape[1]
    is_fine = levels == 0
    coupling = jnp.where(
        fault_faces[:, None, None, :] == 1, fault_flux[None, :, :, None], flux_plus
    )
    lookup = face_source.reshape(-1)

    def beside_values(local_faces, remote):
        source_table = jnp.concatenate(
            [local_faces.reshape(face_width, 4 * elem_count), remote], axis=1
        )
        return jnp.take(source_table, lookup, axis=1).reshape(var_count, -1, 4, elem_count)

    def put_columns(base, update):
        return jnp.where(is_fine, update, base)

    derivs = derivatives(dofs, stiffness, star)
    first_half = integrate(derivs, 0.0, fine_step)
    second_half = integrate(derivs, fine_step, 2.0 * fine_step)
    first_faces = face_values(first_half, projection)
    remote_first = exported(
        jnp.take(first_faces.reshape(face_width, 4 * elem_count), send_source, axis=1)[None]
    )[0]
    beside_first = beside_values(first_faces, remote_first)
    moved = advance(
        dofs,
        first_half,
        first_faces,
        beside_first,
        stiffness,
        projection,
        star,
        flux_minus,
        coupling,
    )
    state_one = put_columns(dofs, moved)
    fine_series = derivatives(state_one, stiffness, star)
    carried = put_columns(second_half, integrate(fine_series, 0.0, fine_step))
    carried_faces = face_values(carried, projection)
    remote_carried = exported(
        jnp.take(carried_faces.reshape(face_width, 4 * elem_count), send_source, axis=1)[None]
    )[0]
    beside_carried = beside_values(carried_faces, remote_carried)
    fine_new = advance(
        state_one,
        carried,
        carried_faces,
        beside_carried,
        stiffness,
        projection,
        star,
        flux_minus,
        coupling,
    )
    whole_step = first_half + second_half
    coarse_new = advance(
        dofs,
        whole_step,
        face_values(whole_step, projection),
        beside_first + beside_carried,
        stiffness,
        projection,
        star,
        flux_minus,
        coupling,
    )
    return put_columns(coarse_new, fine_new)


def solution(mesh):
    return jax.shard_map(
        per_device,
        mesh=mesh,
        in_specs=(
            P(None, None, ("dom", "sub")),
            P(),
            P(),
            P(None, None, None, ("dom", "sub")),
            P(None, None, None, ("dom", "sub")),
            P(None, None, None, ("dom", "sub")),
            P(),
            P(None, ("dom", "sub")),
            P(("dom", "sub")),
            P(None, ("dom", "sub")),
            P(("dom", "sub")),
        ),
        out_specs=P(None, None, ("dom", "sub")),
        check_vma=False,
    )
```

profile of v0, /device:TPU:2, one launch (start us, length us, event | category | flops | bytes accessed | tf_op | source)
XLA Modules:
  0.0 87.7 jit_solution(13629278652495444281)
XLA Ops:
  0.0 0.7 compare_and_fusion.1
  0.9 1.2 %copy.67 = f32[3,9,9,16]{2,1,0,3:T(8,128)S(1)} copy(f32[3,9,9,16]{3,0,2,1:T(4,128)} %param.21) | data formatting | bytes 31104 | tf_op args[3]
  7.6 0.9 %fusion.10 = f32[1,9,56,16]{2,0,3,1:T(1,128)S(1)} fusion(f32[6,1,1,1]{0,1,3,2:T(1,128)S(1)} %copy-done.7, f32[6,9,56,16]{2,1,3,0:T(8,128)S(1)} %fusion.3), kind=kOutput, calls=%fused_computation.35 | convolution fusion | flops 580608 | bytes 225816 | tf_op jit(solution)/shard_map/h,hlui->lui/dot_general | solution.py:67
  10.0 0.6 broadcast_in_dim.51
  10.6 16.5 %all-to-all-start = ((f32[4,1,189,4]{2,3,1,0:T(4,128)}), f32[4,1,189,4]{2,3,1,0:T(4,128)S(1)}, u32[]{:S(2)}, u32[]{:S(2)}) async-start(f32[4,1,189,4]{2,3,1,0:T(4,128)} %broadcast_in_dim.51), calls=%async_computation | async-start | bytes 32768 | tf_op jit(solution)/shard_map/all_to_all | solution.py:17
  27.8 0.9 %fusion.8 = f32[1,9,56,16]{2,0,3,1:T(1,128)S(1)} fusion(f32[6,1,1,1]{0,1,3,2:T(1,128)S(1)} %copy-done.12, f32[6,9,56,16]{2,1,3,0:T(8,128)S(1)} %fusion.3), kind=kOutput, calls=%fused_computation.33 | convolution fusion | flops 580608 | bytes 225816 | tf_op jit(solution)/shard_map/h,hlui->lui/dot_general | solution.py:67
  28.7 0.9 fusion.43
  30.0 0.9 fusion.6
  32.4 8.5 %collective-permute-start.1 = (f32[1,189,1,16]{1,3,2,0:T(8,128)S(1)}, f32[1,189,1,16]{1,3,2,0:T(8,128)S(1)}, u32[]{:S(2)}, u32[]{:S(2)}) collective-permute-start(f32[1,189,1,16]{1,3,2,0:T(8,128)S(1)} %reshape_reshape.6), channel_id=1, source_target_pairs={{4,0},{8,4},{12,8},{16,12},{20,16},{24,20},{28,24},{32,28},{36,32}... | collective-permute-start | bytes 36296 | tf_op jit(solution)/shard_map/ppermute | solution.py:39
  40.9 2.1 %collective-permute-start = (f32[1,189,1,16]{1,3,2,0:T(8,128)S(1)}, f32[1,189,1,16]{1,3,2,0:T(8,128)S(1)}, u32[]{:S(2)}, u32[]{:S(2)}) collective-permute-start(f32[1,189,1,16]{1,3,2,0:T(8,128)S(1)} %reshape_reshape.6), channel_id=1, source_target_pairs={{0,4},{4,8},{8,12},{12,16},{16,20},{20,24},{24,28},{28,32},{32,36}... | collective-permute-start | bytes 36296 | tf_op jit(solution)/shard_map/ppermute | solution.py:38
  43.4 5.9 %collective-permute-done = f32[1,189,1,16]{1,3,2,0:T(8,128)S(1)} collective-permute-done((f32[1,189,1,16]{1,3,2,0:T(8,128)S(1)}, f32[1,189,1,16]{1,3,2,0:T(8,128)S(1)}, u32[]{:S(2)}, u32[]{:S(2)}) %collective-permute-start) | collective-permute-done | bytes 12128 | tf_op jit(solution)/shard_map/ppermute | solution.py:38
  49.3 0.7 gather_fusion.1
  50.3 1.2 %copy.82 = f32[9,21,4,16]{1,0,3,2:T(8,128)} copy(f32[9,21,4,16]{3,2,1,0:T(4,128)S(1)} %reshape.32) | data formatting | bytes 96768 | tf_op jit(solution)/shard_map/reshape | solution.py:132
  51.5 1.7 %fusion.2 = f32[9,21,4,16]{1,0,3,2:T(8,128)S(1)} fusion(f32[4,16,21,9]{2,3,1,0:T(8,128)S(1)} %fusion.43, f32[9,21,4,16]{1,0,3,2:T(8,128)} %copy.82, f32[4,9,9,16]{2,1,3,0:T(8,128)S(1)} %copy.83), kind=kOutput, calls=%fused_computation.9 | convolution fusion | flops 1318464 | bytes 165888 | tf_op jit(solution)/shard_map/fvwe,wjfe->vjfe/dot_general | solution.py:90
  54.4 0.6 fusion.64
  55.5 0.6 fusion.65
  56.5 0.6 fusion.66
  57.6 0.6 fusion.67
  58.7 0.6 convolution_bitcast_fusion.16
  59.5 0.7 fusion.4
  60.8 0.9 fusion.41
  62.6 0.6 broadcast_in_dim.54
  63.3 4.8 %all-to-all-start.1 = ((f32[4,1,189,4]{2,3,1,0:T(4,128)}), f32[4,1,189,4]{2,3,1,0:T(4,128)S(1)}, u32[]{:S(2)}, u32[]{:S(2)}) async-start(f32[4,1,189,4]{2,3,1,0:T(4,128)} %broadcast_in_dim.54), calls=%async_computation.1 | async-start | bytes 32768 | tf_op jit(solution)/shard_map/all_to_all | solution.py:17
  69.4 2.5 %all-to-all-done.1 = f32[4,1,189,4]{2,3,1,0:T(4,128)S(1)} async-done(((f32[4,1,189,4]{2,3,1,0:T(4,128)}), f32[4,1,189,4]{2,3,1,0:T(4,128)S(1)}, u32[]{:S(2)}, u32[]{:S(2)}) %all-to-all-start.1) | async-done | bytes 12128 | tf_op jit(solution)/shard_map/all_to_all | solution.py:17
  72.0 1.9 %collective-permute-start.3 = (f32[1,189,1,16]{1,3,2,0:T(8,128)S(1)}, f32[1,189,1,16]{1,3,2,0:T(8,128)S(1)}, u32[]{:S(2)}, u32[]{:S(2)}) collective-permute-start(f32[1,189,1,16]{1,3,2,0:T(8,128)S(1)} %reshape_reshape.7), channel_id=1, source_target_pairs={{4,0},{8,4},{12,8},{16,12},{20,16},{24,20},{28,24},{32,28},{36,32}... | collective-permute-start | bytes 36296 | tf_op jit(solution)/shard_map/ppermute | solution.py:39
  73.9 2.6 %collective-permute-start.2 = (f32[1,189,1,16]{1,3,2,0:T(8,128)S(1)}, f32[1,189,1,16]{1,3,2,0:T(8,128)S(1)}, u32[]{:S(2)}, u32[]{:S(2)}) collective-permute-start(f32[1,189,1,16]{1,3,2,0:T(8,128)S(1)} %reshape_reshape.7), channel_id=1, source_target_pairs={{0,4},{4,8},{8,12},{12,16},{16,20},{20,24},{24,28},{28,32},{32,36}... | collective-permute-start | bytes 36296 | tf_op jit(solution)/shard_map/ppermute | solution.py:38
  76.5 1.1 %fusion.25 = f32[9,16,56,1]{2,0,3,1:T(8,128)} fusion(f32[3,9,56,16]{2,1,0,3:T(8,128)S(1)} %convolution_bitcast_fusion, f32[3,56,56]{2,1,0:T(8,128)S(1)} %copy-done), kind=kOutput, calls=%fused_computation.57 | convolution fusion | flops 16257024 | bytes 166656 | tf_op jit(solution)/shard_map/utx,uytz->yxz/dot_general | solution.py:88
  77.6 4.7 %collective-permute-done.2 = f32[1,189,1,16]{1,3,2,0:T(8,128)S(1)} collective-permute-done((f32[1,189,1,16]{1,3,2,0:T(8,128)S(1)}, f32[1,189,1,16]{1,3,2,0:T(8,128)S(1)}, u32[]{:S(2)}, u32[]{:S(2)}) %collective-permute-start.2) | collective-permute-done | bytes 12128 | tf_op jit(solution)/shard_map/ppermute | solution.py:38
  82.3 0.7 gather_fusion.3
  83.8 0.6 fusion.1
  85.4 0.6 fusion
  87.0 0.7 fusion.45
  (100 shorter events, 19.1 us)
Async XLA Ops:
  0.0 2.1 %copy-start = (f32[3,56,56]{2,1,0:T(8,128)S(1)}, f32[3,56,56]{2,1,0:T(8,128)}, u32[]{:S(2)}) copy-start(f32[3,56,56]{2,1,0:T(8,128)} %param.19) | copy-start | bytes 112900
  0.0 0.7 copy-start.13
  0.0 0.8 copy-start.10
  0.7 9.1 %copy-start.8 = (pred[4]{0:T(512)(128)(4,1)}, pred[4]{0:T(512)(128)(4,1)S(1)}, u32[]{:S(2)}) copy-start(pred[4]{0:T(512)(128)(4,1)S(1)} %compare_and_fusion.1) | copy-start | bytes 16
  0.9 1.2 %copy-start.2 = (f32[9,56,16]{1,2,0:T(8,128)S(1)}, f32[9,56,16]{1,2,0:T(8,128)}, u32[]{:S(2)}) copy-start(f32[9,56,16]{1,2,0:T(8,128)} %param.18) | copy-start | bytes 96772
  6.9 0.7 copy-start.7
  7.6 0.9 %copy-start.1 = (f32[4,21,56]{2,0,1:T(4,128)S(1)}, f32[4,21,56]{2,0,1:T(4,128)}, u32[]{:S(2)}) copy-start(f32[4,21,56]{2,0,1:T(4,128)} %param.20) | copy-start | bytes 56452
  9.3 17.8 %copy-start.4 = (f32[4,9,9,16]{3,0,2,1:T(4,128)S(1)}, f32[4,9,9,16]{3,0,2,1:T(4,128)}, u32[]{:S(2)}) copy-start(f32[4,9,9,16]{3,0,2,1:T(4,128)} %param.22) | copy-start | bytes 62212
  10.6 16.5 %copy-start.11 = (s32[4,16]{1,0:T(4,128)S(1)}, s32[4,16]{1,0:T(4,128)}, u32[]{:S(2)}) copy-start(s32[4,16]{1,0:T(4,128)} %param.25) | copy-start | bytes 772
  10.6 21.8 %all-to-all-start = ((f32[4,1,189,4]{2,3,1,0:T(4,128)}), f32[4,1,189,4]{2,3,1,0:T(4,128)S(1)}, u32[]{:S(2)}, u32[]{:S(2)}) async-start(f32[4,1,189,4]{2,3,1,0:T(4,128)} %broadcast_in_dim.51), calls=%async_computation | async-start | bytes 32768 | tf_op jit(solution)/shard_map/all_to_all | solution.py:17
  27.1 0.7 copy-start.12
  31.3 0.9 %copy-start.5 = (f32[4,9,9,16]{3,0,2,1:T(4,128)S(1)}, f32[4,9,9,16]{3,0,2,1:T(4,128)}, u32[]{:S(2)}) copy-start(f32[4,9,9,16]{3,0,2,1:T(4,128)} %param.23) | copy-start | bytes 62212
  31.3 0.9 %copy-start.6 = (f32[9,9]{1,0:T(8,128)S(1)}, f32[9,9]{1,0:T(8,128)}, u32[]{:S(2)}) copy-start(f32[9,9]{1,0:T(8,128)} %param.24) | copy-start | bytes 976
  32.4 10.6 %copy-start.14 = (s32[16]{0:T(128)S(1)}, s32[16]{0:T(128)}, u32[]{:S(2)}) copy-start(s32[16]{0:T(128)} %param.26) | copy-start | bytes 196
  32.4 10.9 %collective-permute-start.1 = (f32[1,189,1,16]{1,3,2,0:T(8,128)S(1)}, f32[1,189,1,16]{1,3,2,0:T(8,128)S(1)}, u32[]{:S(2)}, u32[]{:S(2)}) collective-permute-start(f32[1,189,1,16]{1,3,2,0:T(8,128)S(1)} %reshape_reshape.6), channel_id=1, source_target_pairs={{4,0},{8,4},{12,8},{16,12},{20,16},{24,20},{28,24},{32,28},{36,32}... | collective-permute-start | bytes 36296 | tf_op jit(solution)/shard_map/ppermute | solution.py:39
  40.9 8.4 %collective-permute-start = (f32[1,189,1,16]{1,3,2,0:T(8,128)S(1)}, f32[1,189,1,16]{1,3,2,0:T(8,128)S(1)}, u32[]{:S(2)}, u32[]{:S(2)}) collective-permute-start(f32[1,189,1,16]{1,3,2,0:T(8,128)S(1)} %reshape_reshape.6), channel_id=1, source_target_pairs={{0,4},{4,8},{8,12},{12,16},{16,20},{20,24},{24,28},{28,32},{32,36}... | collective-permute-start | bytes 36296 | tf_op jit(solution)/shard_map/ppermute | solution.py:38
  62.0 0.6 copy-start.9
  63.3 8.7 %all-to-all-start.1 = ((f32[4,1,189,4]{2,3,1,0:T(4,128)}), f32[4,1,189,4]{2,3,1,0:T(4,128)S(1)}, u32[]{:S(2)}, u32[]{:S(2)}) async-start(f32[4,1,189,4]{2,3,1,0:T(4,128)} %broadcast_in_dim.54), calls=%async_computation.1 | async-start | bytes 32768 | tf_op jit(solution)/shard_map/all_to_all | solution.py:17
  72.0 5.6 %collective-permute-start.3 = (f32[1,189,1,16]{1,3,2,0:T(8,128)S(1)}, f32[1,189,1,16]{1,3,2,0:T(8,128)S(1)}, u32[]{:S(2)}, u32[]{:S(2)}) collective-permute-start(f32[1,189,1,16]{1,3,2,0:T(8,128)S(1)} %reshape_reshape.7), channel_id=1, source_target_pairs={{4,0},{8,4},{12,8},{16,12},{20,16},{24,20},{28,24},{32,28},{36,32}... | collective-permute-start | bytes 36296 | tf_op jit(solution)/shard_map/ppermute | solution.py:39
  73.9 8.4 %collective-permute-start.2 = (f32[1,189,1,16]{1,3,2,0:T(8,128)S(1)}, f32[1,189,1,16]{1,3,2,0:T(8,128)S(1)}, u32[]{:S(2)}, u32[]{:S(2)}) collective-permute-start(f32[1,189,1,16]{1,3,2,0:T(8,128)S(1)} %reshape_reshape.7), channel_id=1, source_target_pairs={{0,4},{4,8},{8,12},{12,16},{16,20},{20,24},{24,28},{28,32},{32,36}... | collective-permute-start | bytes 36296 | tf_op jit(solution)/shard_map/ppermute | solution.py:38
  86.1 0.9 %copy-start.3 = (f32[9,16,56,1]{2,0,3,1:T(8,128)S(1)}, f32[9,16,56,1]{2,0,3,1:T(8,128)}, u32[]{:S(2)}) copy-start(f32[9,16,56,1]{2,0,3,1:T(8,128)} %fusion.25) | copy-start | bytes 96772
where the time goes:
time: 88.2 us; the launch traced here: 87.7 us
  starting transfers between devices  36.4 us (41%)
  matrix products  25.2 us (29%)
  waiting for transfers between devices  13.1 us (15%)
  local copies, waits for them, and re-layouts  10.2 us (12%)
  other arithmetic  2.23 us (3%)
    all_to_all x2, starting transfers between devices, from_everyone(): return lax.all_to_all(copies, axis, split_axis=0, concat_axis=0, tiled=True)  21.3 us
    ppermute x2, waiting for transfers between devices, padded(): before = lax.ppermute(last, axis, up)  10.6 us
    ppermute x2, starting transfers between devices, padded(): after = lax.ppermute(first, axis, down)  10.4 us
    dot_general x10, matrix products, derivatives(): jnp.einsum('usij,uifj->sfj', star_contribution, time_slopes, precision=ex...  6.01 us
    dot_general x10, matrix products, derivatives(): jnp.einsum('dmn,wne->dwme', stiffness, taylor_series[-1], precision=exact...  4.75 us
    ppermute x2, starting transfers between devices, padded(): before = lax.ppermute(last, axis, up)  4.73 us
    dot_general x3, matrix products, advance(): jnp.einsum('fvwe,wjfe->vjfe', coupling_part, beside, precision=exact_refe...  2.94 us
    unnamed x37, local copies, waits for them, and re-layouts  2.91 us
  transfers between devices with their start and end apart: 6, of which 3 were waited for; matrix products, arithmetic and copies ran while one was open for 8% of the time, Pallas kernels for 0%

commit v1 on v0

v1 whole, which is shorter than its diff:
```python
import functools
import math

import jax
import jax.numpy as jnp
from jax import lax
from jax.experimental import pallas as pl
from jax.experimental.pallas import tpu as pltpu
from jax.sharding import PartitionSpec as P

ORDER = 6
TAU = 0.75
V = 9
M = 56
J = 21
E = 16
SLOTS = 12
MESH = pl.DeviceIdType.MESH
F32 = jnp.float32
BF16 = jnp.bfloat16


def taylor_weights(start_time, stop_time):
    return [
        (stop_time ** (k + 1) - start_time ** (k + 1)) / math.factorial(k + 1)
        for k in range(ORDER)
    ]


FIRST = taylor_weights(0.0, TAU)
SECOND = taylor_weights(TAU, 2.0 * TAU)


def split(x):
    hi = x.astype(BF16)
    return hi, (x - hi.astype(F32)).astype(BF16)


def lhs3(x):
    hi, lo = split(x)
    return jnp.concatenate([hi, lo, hi], axis=1)


def rhs3(x):
    hi, lo = split(x)
    return jnp.concatenate([hi, hi, lo], axis=0)


def stack2(x):
    hi, lo = split(x)
    return jnp.concatenate([hi, lo], axis=0)


def dot(a, b):
    return jnp.dot(a, b, preferred_element_type=F32)


def lanes(shape=(8, 128)):
    return lax.broadcasted_iota(jnp.int32, shape, 1)


def rows(shape=(8, 128)):
    return lax.broadcasted_iota(jnp.int32, shape, 0)


def roll(x, shift):
    return pltpu.roll(x, shift % 128, 1)


def swap_blocks(a):
    lane = lanes()
    low = lane < 64
    even = (lane // 32) % 2 == 0
    p0 = jnp.where(low, a[0], roll(a[2], 64))
    p2 = jnp.where(low, roll(a[0], 64), a[2])
    p1 = jnp.where(low, a[1], roll(a[3], 64))
    p3 = jnp.where(low, roll(a[1], 64), a[3])
    return [
        jnp.where(even, p0, roll(p1, 32)),
        jnp.where(even, roll(p0, -32), p1),
        jnp.where(even, p2, roll(p3, 32)),
        jnp.where(even, roll(p2, -32), p3),
    ]


def to_table(faces):
    lane = lanes()
    ends = (lane >= J) & (lane < 32)
    more = (lane >= 32 + J) & (lane < 42 + J)
    first, second = [], []
    for half in range(2):
        part = [faces[8 * w : 8 * w + 8, 128 * half : 128 * half + 128] for w in range(V)]
        one = swap_blocks(part[0:4])
        two = swap_blocks(part[4:8])
        for b in range(4):
            kept = jnp.where(ends, roll(part[8], J - 32 * b), one[b])
            first.append(jnp.where(more, roll(part[8], 42 - 32 * b), kept))
            second.append(two[b])
    return jnp.concatenate(first, axis=0), jnp.concatenate(second, axis=0)


def from_table(first, second):
    lane = lanes()
    halves = []
    for half in range(2):
        one = [first[32 * half + 8 * b : 32 * half + 8 * b + 8] for b in range(4)]
        two = [second[32 * half + 8 * b : 32 * half + 8 * b + 8] for b in range(4)]
        last = jnp.zeros((8, 128), F32)
        for b in range(4):
            inside = lane - 32 * b
            last = jnp.where((inside >= 0) & (inside < 11), roll(one[b], 32 * b - J), last)
            last = jnp.where((inside >= 11) & (inside < J), roll(one[b], 32 * b - 42), last)
        halves.append(swap_blocks(one) + swap_blocks(two) + [last])
    return [jnp.concatenate([halves[0][w], halves[1][w]], axis=1) for w in range(V)]


def kernel(
    n_dom,
    n_sub,
    levels_ref,
    source_ref,
    send_ref,
    fault_flux_ref,
    fault_faces_ref,
    dofs_hbm,
    stiff_hbm,
    proj_hbm,
    star_hbm,
    minus_hbm,
    plus_hbm,
    out_ref,
    dofs_ref,
    stiff_ref,
    proj_ref,
    star_ref,
    minus_ref,
    plus_ref,
    block_ref,
    pt_ref,
    x_ref,
    row_ref,
    wd_ref,
    wv_ref,
    pw_ref,
    pt3_ref,
    cs_ref,
    cm_ref,
    cc_ref,
    flux_ref,
    msg_ref,
    recv_ref,
    in_sem,
    send_sem,
    recv_sem,
):
    dom = lax.axis_index("dom")
    sub = lax.axis_index("sub")
    peers = []
    for delta in (-1, 1, 0):
        for turn in (2, 1, 3, 0):
            if delta == 0 and turn == 0:
                continue
            peers.append((delta, lax.rem(dom + delta + n_dom, n_dom), lax.rem(sub + turn, n_sub)))

    barrier = pltpu.get_barrier_semaphore()
    for _, to_dom, to_sub in peers:
        pl.semaphore_signal(barrier, inc=1, device_id=(to_dom, to_sub), device_id_type=MESH)

    loads = [
        pltpu.make_async_copy(src, dst, in_sem.at[i])
        for i, (src, dst) in enumerate(
            (
                (stiff_hbm, stiff_ref),
                (star_hbm, star_ref),
                (dofs_hbm, dofs_ref),
                (proj_hbm, proj_ref),
                (minus_hbm, minus_ref),
                (plus_hbm, plus_ref),
            )
        )
    ]
    for load in loads:
        load.start()

    block_ref[...] = jnp.zeros(block_ref.shape, F32)
    pt_ref[...] = jnp.zeros(pt_ref.shape, F32)
    x_ref[...] = jnp.zeros(x_ref.shape, F32)
    row_ref[...] = jnp.zeros(row_ref.shape, F32)

    loads[0].wait()
    for d in range(3):
        block_ref[d, 0:M, 0:M] = stiff_ref[d]
        block_ref[d, 64 : 64 + M, 64 : 64 + M] = stiff_ref[d]
    for d in range(3):
        block = block_ref[d]
        wd_ref[:, 128 * d : 128 * d + 128] = rhs3(block.T)
        wv_ref[:, 128 * d : 128 * d + 128] = rhs3(block)

    def spread(make_row, groups, part_width, fill, coef_ref):
        width = 128 * coef_ref.shape[3] // 128
        k = lax.broadcasted_iota(jnp.int32, (128, width), 0) % 64
        lane = lax.broadcasted_iota(jnp.int32, (128, width), 1)
        group = lane // (2 * part_width)
        half = (lane // part_width) % 2
        hit = (k // E == group) & ((k % E) // 8 == half) & (lane % part_width < fill)
        repeat = hit.astype(F32).astype(BF16)
        keep = (lanes() % 8 == rows()).astype(F32)
        for v in range(V):
            row = make_row(v)
            high = row.astype(BF16).astype(F32)
            row_ref[v, 0:V, 0 : groups * E] = high
            row_ref[v, 0:V, 64 : 64 + groups * E] = row - high
        for v in range(V):
            left = jnp.concatenate(
                [jnp.broadcast_to(row_ref[v, w : w + 1, :], (8, 128)) * keep for w in range(V)],
                axis=0,
            ).astype(BF16)
            coef_ref[v] = dot(left, repeat).reshape(V, 8, width)

    loads[1].wait()
    spread(
        lambda v: jnp.concatenate([star_ref[v, :, d, :] for d in range(3)], axis=1),
        3,
        64,
        M,
        cs_ref,
    )

    loads[2].wait()
    for v in range(V):
        x_ref[8 * v : 8 * v + 8, 0:M] = dofs_ref[v, 0:8, :]
        x_ref[8 * v : 8 * v + 8, 64 : 64 + M] = dofs_ref[v, 8:16, :]

    def contract(coef_ref, field, v):
        return (coef_ref[v] * field).sum(axis=0)

    def with_star(weights_ref, left):
        field = dot(left, weights_ref[...]).reshape(V, 8, 384)
        result = []
        for v in range(V):
            total = contract(cs_ref, field, v)
            result.append(total[:, 0:128] + total[:, 128:256] + total[:, 256:384])
        return jnp.concatenate(result, axis=0)

    def series(start, want_second):
        current = start
        first = FIRST[0] * current
        second = SECOND[0] * current if want_second else None
        for k in range(1, ORDER):
            current = with_star(wd_ref, lhs3(current))
            first = first + FIRST[k] * current
            if want_second:
                second = second + SECOND[k] * current
        return first, second

    dofs = x_ref[...]
    first_half, second_half = series(dofs, True)

    loads[3].wait()
    for f in range(4):
        for half in range(2):
            at = 64 * f + 32 * half
            pt_ref[at : at + J, 64 * half : 64 * half + M] = proj_ref[:, f, :]
    pt = pt_ref[...]
    pw_ref[...] = rhs3(pt.T)
    pt3_ref[...] = rhs3(pt)

    row = rows((8, 256))
    lane = lanes((8, 256))
    wanted = jnp.full((8, 256), -1, jnp.int32)
    for s in range(4):
        wanted = jnp.where(row % 4 == s, send_ref[s], wanted)
    pick_send = ((lane % 64 == wanted) & (lane // 128 == row // 4)).astype(F32).astype(BF16)

    local_rows, remote_rows = [], []
    row = rows()
    lane = lanes()
    lane2 = lanes((8, 192)) % 96
    for f in range(4):
        for half in range(2):
            wanted = jnp.full((8, 128), -1, jnp.int32)
            for i in range(8):
                wanted = jnp.where(row == i, source_ref[f, 8 * half + i], wanted)
            local_rows.append((lane % 64 == wanted).astype(F32))
            far = wanted - 64
            code = jnp.where(far >= 0, (far // 4) * 8 + far % 4, -8)
            code = jnp.concatenate([code, code[:, 0:64]], axis=1)
            remote_rows.append((code, lane2))
    pick_local = jnp.concatenate(local_rows, axis=0).astype(BF16)
    pick_remote = jnp.concatenate(
        [(at == code + 4 * q).astype(F32) for q in range(2) for code, at in remote_rows], axis=0
    ).astype(BF16)

    fine = jnp.zeros((8, 128), jnp.int32)
    for e in range(E):
        here = (row == e % 8) & (lane // 64 == e // 8)
        fine = jnp.where(here & (levels_ref[e] == 0), 1, fine)
    fine = jnp.concatenate([fine] * V, axis=0) == 1

    def start_exchange(turn, table):
        stacked = jnp.concatenate([stack2(table[0]), stack2(table[1])], axis=0)
        message = dot(pick_send, stacked)
        msg_ref[turn] = message
        recv_ref[turn, 4 + sub] = message
        copies = []
        for delta, to_dom, to_sub in peers:
            copies.append(
                pltpu.make_async_remote_copy(
                    src_ref=msg_ref.at[turn],
                    dst_ref=recv_ref.at[turn, 4 * (1 - delta) + sub],
                    send_sem=send_sem.at[turn, len(copies)],
                    recv_sem=recv_sem.at[turn, 4 * (1 - delta) + sub],
                    device_id=(to_dom, to_sub),
                    device_id_type=MESH,
                )
            )
        return copies

    def finish_exchange(turn, copies):
        for delta in (-1, 0, 1):
            for shift in range(4):
                if delta == 0 and shift == 0:
                    continue
                slot = 4 * (1 - delta) + lax.rem(sub + shift, n_sub)
                pltpu.make_async_remote_copy(
                    src_ref=msg_ref.at[turn],
                    dst_ref=recv_ref.at[turn, slot],
                    send_sem=send_sem.at[turn, 0],
                    recv_sem=recv_sem.at[turn, slot],
                    device_id=(dom, lax.rem(sub + 1, n_sub)),
                    device_id_type=MESH,
                ).wait_recv()

    def local_part(table):
        return dot(pick_local, jnp.concatenate([stack2(table[0]), stack2(table[1])], axis=1))

    def beside_faces(turn, near):
        far = dot(pick_remote, stack2(recv_ref[turn].reshape(8 * SLOTS, 128)))
        faces = from_table(near[:, 0:128] + far[0:64], near[:, 128:256] + far[64:128])
        return jnp.concatenate(faces, axis=0).reshape(V, 8, 256)

    left = lhs3(first_half)
    faces = dot(left, pw_ref[...])
    table = to_table(faces)
    copies = start_exchange(0, table)
    pl.semaphore_wait(barrier, len(peers))
    for copy in copies:
        copy.start()
    sent = list(copies)

    loads[4].wait()
    spread(
        lambda v: jnp.concatenate([minus_ref[v, :, f, :] for f in range(4)], axis=1),
        4,
        32,
        J,
        cm_ref,
    )
    loads[5].wait()
    on_fault = jnp.concatenate([fault_faces_ref[f : f + 1, :] for f in range(4)], axis=1) == 1

    def coupling_row(v):
        plus = jnp.concatenate([plus_ref[v, :, f, :] for f in range(4)], axis=1)
        w_at = rows((V, 4 * E))
        friction = jnp.zeros((V, 4 * E), F32)
        for w in range(V):
            friction = jnp.where(w_at == w, fault_flux_ref[v, w], friction)
        return jnp.where(jnp.broadcast_to(on_fault, (V, 4 * E)), friction, plus)

    spread(coupling_row, 4, 32, J, cc_ref)

    def own_side(left, faces):
        volume = with_star(wv_ref, left)
        field = faces.reshape(V, 8, 256)
        for v in range(V):
            flux_ref[8 * v : 8 * v + 8, :] = contract(cm_ref, field, v)
        return volume

    def far_side(base, turn, near):
        field = beside_faces(turn, near)
        total = jnp.concatenate([contract(cc_ref, field, v) for v in range(V)], axis=0)
        return base - dot(lhs3(total + flux_ref[...]), pt3_ref[...])

    near = local_part(table)
    base = dofs + own_side(left, faces)
    finish_exchange(0, copies)
    moved = far_side(base, 0, near)

    again, _ = series(moved, False)
    carried = jnp.where(fine, again, second_half)
    left = lhs3(carried)
    faces = dot(left, pw_ref[...])
    table = to_table(faces)
    copies = start_exchange(1, table)
    for copy in copies:
        copy.start()
    sent += copies
    near = local_part(table)
    base = moved + own_side(left, faces)
    finish_exchange(1, copies)
    after = far_side(base, 1, near)
    for v in range(V):
        out_ref[v, 0:8, :] = after[8 * v : 8 * v + 8, 0:M]
        out_ref[v, 8:16, :] = after[8 * v : 8 * v + 8, 64 : 64 + M]
    for copy in sent:
        copy.wait_send()


def per_device(
    n_dom,
    n_sub,
    dofs,
    stiffness,
    projection,
    star,
    flux_minus,
    flux_plus,
    fault_flux,
    fault_faces,
    levels,
    face_source,
    send_source,
):
    smem = pl.BlockSpec(memory_space=pltpu.SMEM)
    vmem = pl.BlockSpec(memory_space=pltpu.VMEM)
    hbm = pl.BlockSpec(memory_space=pl.ANY)
    result = pl.pallas_call(
        functools.partial(kernel, n_dom, n_sub),
        out_shape=jax.ShapeDtypeStruct((V, E, M), F32),
        in_specs=[smem] * 4 + [vmem] + [hbm] * 6,
        out_specs=vmem,
        scratch_shapes=[
            pltpu.VMEM((V, E, M), F32),
            pltpu.VMEM((3, M, M), F32),
            pltpu.VMEM((J, 4, M), F32),
            pltpu.VMEM((V, V, 3, E), F32),
            pltpu.VMEM((V, V, 4, E), F32),
            pltpu.VMEM((V, V, 4, E), F32),
            pltpu.VMEM((3, 128, 128), F32),
            pltpu.VMEM((256, 128), F32),
            pltpu.VMEM((72, 128), F32),
            pltpu.VMEM((V, 16, 128), F32),
            pltpu.VMEM((384, 384), BF16),
            pltpu.VMEM((384, 384), BF16),
            pltpu.VMEM((384, 256), BF16),
            pltpu.VMEM((768, 128), BF16),
            pltpu.VMEM((V, V, 8, 384), F32),
            pltpu.VMEM((V, V, 8, 256), F32),
            pltpu.VMEM((V, V, 8, 256), F32),
            pltpu.VMEM((72, 256), F32),
            pltpu.VMEM((2, 8, 128), F32),
            pltpu.VMEM((2, SLOTS, 8, 128), F32),
            pltpu.SemaphoreType.DMA((6,)),
            pltpu.SemaphoreType.DMA((2, SLOTS)),
            pltpu.SemaphoreType.DMA((2, SLOTS)),
        ],
        compiler_params=pltpu.CompilerParams(collective_id=0, has_side_effects=True),
    )(
        levels,
        face_source,
        send_source,
        fault_flux,
        fault_faces,
        jnp.transpose(dofs, (0, 2, 1)),
        stiffness,
        jnp.transpose(projection, (1, 0, 2)),
        jnp.transpose(star, (1, 2, 0, 3)),
        jnp.transpose(flux_minus, (1, 2, 0, 3)),
        jnp.transpose(flux_plus, (1, 2, 0, 3)),
    )
    return jnp.transpose(result, (0, 2, 1))


def solution(mesh):
    return jax.shard_map(
        functools.partial(per_device, mesh.shape["dom"], mesh.shape["sub"]),
        mesh=mesh,
        in_specs=(
            P(None, None, ("dom", "sub")),
            P(),
            P(),
            P(None, None, None, ("dom", "sub")),
            P(None, None, None, ("dom", "sub")),
            P(None, None, None, ("dom", "sub")),
            P(),
            P(None, ("dom", "sub")),
            P(("dom", "sub")),
            P(None, ("dom", "sub")),
            P(("dom", "sub")),
        ),
        out_specs=P(None, None, ("dom", "sub")),
        check_vma=False,
    )
```

time: 88.2 us -> 37.4 us (0.42)
  the two profiles are of different devices: /device:TPU:2 before, /device:TPU:1 now
where the time goes in v1:
time: 37.4 us; the launch traced here: 36.9 us
  Pallas kernels  35.3 us (94%)
  local copies, waits for them, and re-layouts  1.52 us (4%)
    pallas_call x1, Pallas kernels, per_device(): pl.pallas_call(functools.partial(kernel, n_dom, n_sub), out_shape=jax.Sha...  35.3 us
    unnamed x1, local copies, waits for them, and re-layouts  1.52 us

profile of v1, /device:TPU:1, one launch (start us, length us, event | category | flops | bytes accessed | tf_op | source)
XLA Modules:
  0.0 36.9 jit_solution(7893322374053273788)
XLA Ops:
  0.0 35.3 %shard_map.109 = f32[9,16,56]{2,1,0:T(8,128)} custom-call(s32[16]{0:T(128)} %levels_ref.1, s32[4,16]{1,0:T(4,128)} %source_ref.1, s32[4]{0:T(128)} %send_ref.1, f32[9,9]{1,0:T(8,128)} %fault_flux_ref.1, s32[4,16]{1,0:T(4,128)} %fault_faces_ref.1, f32[9,16,56]{2,1,0:T(8,128)} %bitcast.10, f32[3,56,56]{2,1,0:T(8,128)} %stiff_hbm.1, f32[21,4,56]{2,1,0:T(4,128)} %bitcast.11, ...), custom_call_target="tpu_custom_call" | custom-call | tf_op jit(solution)/shard_map/pallas_call | solution.py:427
  35.4 1.5 %copy.13 = f32[9,56,16]{1,2,0:T(8,128)} copy(f32[9,56,16]{1,2,0:T(8,128)} %bitcast.6) | data formatting | bytes 64512

commit v2 on v1

--- a/solution.py
+++ b/solution.py
@@ -15,6 +15,7 @@
 J = 21
 E = 16
 SLOTS = 12
+VMEM_LIMIT = 24 * 2**20
 MESH = pl.DeviceIdType.MESH
 F32 = jnp.float32
 BF16 = jnp.bfloat16
@@ -117,11 +118,11 @@
 def kernel(
     n_dom,
     n_sub,
-    levels_ref,
-    source_ref,
-    send_ref,
-    fault_flux_ref,
-    fault_faces_ref,
+    levels_hbm,
+    source_hbm,
+    send_hbm,
+    fault_flux_hbm,
+    fault_faces_hbm,
     dofs_hbm,
     stiff_hbm,
     proj_hbm,
@@ -129,6 +130,11 @@
     minus_hbm,
     plus_hbm,
     out_ref,
+    levels_ref,
+    source_ref,
+    send_ref,
+    fault_flux_ref,
+    fault_faces_ref,
     dofs_ref,
     stiff_ref,
     proj_ref,
@@ -176,6 +182,11 @@
                 (proj_hbm, proj_ref),
                 (minus_hbm, minus_ref),
                 (plus_hbm, plus_ref),
+                (levels_hbm, levels_ref),
+                (source_hbm, source_ref),
+                (send_hbm, send_ref),
+                (fault_flux_hbm, fault_flux_ref),
+                (fault_faces_hbm, fault_faces_ref),
             )
         )
     ]
@@ -265,6 +276,8 @@
     pw_ref[...] = rhs3(pt.T)
     pt3_ref[...] = rhs3(pt)
 
+    for i in (6, 7, 8):
+        loads[i].wait()
     row = rows((8, 256))
     lane = lanes((8, 256))
     wanted = jnp.full((8, 256), -1, jnp.int32)
@@ -356,7 +369,8 @@
         J,
         cm_ref,
     )
-    loads[5].wait()
+    for i in (5, 9, 10):
+        loads[i].wait()
     on_fault = jnp.concatenate([fault_faces_ref[f : f + 1, :] for f in range(4)], axis=1) == 1
 
     def coupling_row(v):
@@ -397,13 +411,13 @@
     sent += copies
     near = local_part(table)
     base = moved + own_side(left, faces)
+    for copy in sent:
+        copy.wait_send()
     finish_exchange(1, copies)
     after = far_side(base, 1, near)
     for v in range(V):
         out_ref[v, 0:8, :] = after[8 * v : 8 * v + 8, 0:M]
         out_ref[v, 8:16, :] = after[8 * v : 8 * v + 8, 64 : 64 + M]
-    for copy in sent:
-        copy.wait_send()
 
 
 def per_device(
@@ -421,15 +435,19 @@
     face_source,
     send_source,
 ):
-    smem = pl.BlockSpec(memory_space=pltpu.SMEM)
     vmem = pl.BlockSpec(memory_space=pltpu.VMEM)
-    hbm = pl.BlockSpec(memory_space=pl.ANY)
+    hbm = pl.BlockSpec(memory_space=pltpu.HBM)
     result = pl.pallas_call(
         functools.partial(kernel, n_dom, n_sub),
-        out_shape=jax.ShapeDtypeStruct((V, E, M), F32),
-        in_specs=[smem] * 4 + [vmem] + [hbm] * 6,
+        out_shape=pltpu.VMEM((V, E, M), F32),
+        in_specs=[hbm] * 11,
         out_specs=vmem,
         scratch_shapes=[
+            pltpu.SMEM((E,), jnp.int32),
+            pltpu.SMEM((4, E), jnp.int32),
+            pltpu.SMEM((4,), jnp.int32),
+            pltpu.SMEM((V, V), F32),
+            pltpu.VMEM((4, E), jnp.int32),
             pltpu.VMEM((V, E, M), F32),
             pltpu.VMEM((3, M, M), F32),
             pltpu.VMEM((J, 4, M), F32),
@@ -450,12 +468,17 @@
             pltpu.VMEM((72, 256), F32),
             pltpu.VMEM((2, 8, 128), F32),
             pltpu.VMEM((2, SLOTS, 8, 128), F32),
-            pltpu.SemaphoreType.DMA((6,)),
+            pltpu.SemaphoreType.DMA((11,)),
             pltpu.SemaphoreType.DMA((2, SLOTS)),
             pltpu.SemaphoreType.DMA((2, SLOTS)),
         ],
-        compiler_params=pltpu.CompilerParams(collective_id=0, has_side_effects=True),
+        compiler_params=pltpu.CompilerParams(
+            collective_id=0, has_side_effects=True, vmem_limit_bytes=VMEM_LIMIT
+        ),
     )(
+        *(
+            pltpu.with_memory_space_constraint(x, pltpu.HBM)
+            for x in (
         levels,
         face_source,
         send_source,
@@ -467,6 +490,8 @@
         jnp.transpose(star, (1, 2, 0, 3)),
         jnp.transpose(flux_minus, (1, 2, 0, 3)),
         jnp.transpose(flux_plus, (1, 2, 0, 3)),
+                )
+        )
     )
     return jnp.transpose(result, (0, 2, 1))
 

time: 37.4 us -> 35 us (0.936)
  Pallas kernels: 35.3 us -> 33.9 us
  local copies, waits for them, and re-layouts: 1.52 us -> 0.64 us
    pallas_call x1, Pallas kernels: 35.3 us -> 33.9 us  [per_device(): pl.pallas_call(functools.partial(kernel, n_dom, n_sub), out_shape=pltpu.V...]
    unnamed x1, local copies, waits for them, and re-layouts: 1.52 us -> 0.64 us
where the time goes in v2:
time: 35 us; the launch traced here: 34.5 us
  Pallas kernels  33.9 us (97%)
  local copies, waits for them, and re-layouts  0.64 us (2%)
    pallas_call x1, Pallas kernels, per_device(): pl.pallas_call(functools.partial(kernel, n_dom, n_sub), out_shape=pltpu.V...  33.9 us

profile of v2, /device:TPU:1, one launch (start us, length us, event | category | flops | bytes accessed | tf_op | source)
XLA Modules:
  0.0 34.5 jit_solution(17656149173886961298)
XLA Ops:
  0.0 33.9 %shard_map.109 = f32[9,16,56]{2,1,0:T(8,128)S(1)} custom-call(s32[16]{0:T(128)} %levels_hbm.1, s32[4,16]{1,0:T(4,128)} %source_hbm.1, s32[4]{0:T(128)} %send_hbm.1, f32[9,9]{1,0:T(8,128)} %fault_flux_hbm.1, s32[4,16]{1,0:T(4,128)} %fault_faces_hbm.1, f32[9,16,56]{2,1,0:T(8,128)} %bitcast.10, f32[3,56,56]{2,1,0:T(8,128)} %stiff_hbm.1, f32[21,4,56]{2,1,0:T(4,128)} %bitcast.11, ...), custom_call_target="tpu_custom_call" | custom-call | tf_op jit(solution)/shard_map/pallas_call | solution.py:440
  33.9 0.6 %copy.13 = f32[9,56,16]{1,2,0:T(8,128)} copy(f32[9,56,16]{1,2,0:T(8,128)S(1)} %bitcast.6) | data formatting | bytes 64512

commit v3 on v2

--- a/solution.py
+++ b/solution.py
@@ -264,9 +264,6 @@
                 second = second + SECOND[k] * current
         return first, second
 
-    dofs = x_ref[...]
-    first_half, second_half = series(dofs, True)
-
     loads[3].wait()
     for f in range(4):
         for half in range(2):
@@ -310,39 +307,39 @@
         fine = jnp.where(here & (levels_ref[e] == 0), 1, fine)
     fine = jnp.concatenate([fine] * V, axis=0) == 1
 
+    dofs = x_ref[...]
+    first_half, second_half = series(dofs, True)
+
     def start_exchange(turn, table):
         stacked = jnp.concatenate([stack2(table[0]), stack2(table[1])], axis=0)
         message = dot(pick_send, stacked)
         msg_ref[turn] = message
         recv_ref[turn, 4 + sub] = message
-        copies = []
-        for delta, to_dom, to_sub in peers:
-            copies.append(
-                pltpu.make_async_remote_copy(
-                    src_ref=msg_ref.at[turn],
-                    dst_ref=recv_ref.at[turn, 4 * (1 - delta) + sub],
-                    send_sem=send_sem.at[turn, len(copies)],
-                    recv_sem=recv_sem.at[turn, 4 * (1 - delta) + sub],
-                    device_id=(to_dom, to_sub),
-                    device_id_type=MESH,
-                )
+        return [
+            pltpu.make_async_remote_copy(
+                src_ref=msg_ref.at[turn],
+                dst_ref=recv_ref.at[turn, 4 * (1 - delta) + sub],
+                send_sem=send_sem.at[turn],
+                recv_sem=recv_sem.at[turn],
+                device_id=(to_dom, to_sub),
+                device_id_type=MESH,
             )
-        return copies
+            for delta, to_dom, to_sub in peers
+        ]
+
+    def all_messages(turn):
+        some = recv_ref.at[turn, pl.ds(0, len(peers))]
+        return pltpu.make_async_remote_copy(
+            src_ref=some,
+            dst_ref=some,
+            send_sem=send_sem.at[turn],
+            recv_sem=recv_sem.at[turn],
+            device_id=(dom, lax.rem(sub + 1, n_sub)),
+            device_id_type=MESH,
+        )
 
     def finish_exchange(turn, copies):
-        for delta in (-1, 0, 1):
-            for shift in range(4):
-                if delta == 0 and shift == 0:
-                    continue
-                slot = 4 * (1 - delta) + lax.rem(sub + shift, n_sub)
-                pltpu.make_async_remote_copy(
-                    src_ref=msg_ref.at[turn],
-                    dst_ref=recv_ref.at[turn, slot],
-                    send_sem=send_sem.at[turn, 0],
-                    recv_sem=recv_sem.at[turn, slot],
-                    device_id=(dom, lax.rem(sub + 1, n_sub)),
-                    device_id_type=MESH,
-                ).wait_recv()
+        all_messages(turn).wait_recv()
 
     def local_part(table):
         return dot(pick_local, jnp.concatenate([stack2(table[0]), stack2(table[1])], axis=1))
@@ -359,7 +356,6 @@
     pl.semaphore_wait(barrier, len(peers))
     for copy in copies:
         copy.start()
-    sent = list(copies)
 
     loads[4].wait()
     spread(
@@ -408,11 +404,10 @@
     copies = start_exchange(1, table)
     for copy in copies:
         copy.start()
-    sent += copies
     near = local_part(table)
     base = moved + own_side(left, faces)
-    for copy in sent:
-        copy.wait_send()
+    all_messages(0).wait_send()
+    all_messages(1).wait_send()
     finish_exchange(1, copies)
     after = far_side(base, 1, near)
     for v in range(V):
@@ -469,8 +464,8 @@
             pltpu.VMEM((2, 8, 128), F32),
             pltpu.VMEM((2, SLOTS, 8, 128), F32),
             pltpu.SemaphoreType.DMA((11,)),
-            pltpu.SemaphoreType.DMA((2, SLOTS)),
-            pltpu.SemaphoreType.DMA((2, SLOTS)),
+            pltpu.SemaphoreType.DMA((2,)),
+            pltpu.SemaphoreType.DMA((2,)),
         ],
         compiler_params=pltpu.CompilerParams(
             collective_id=0, has_side_effects=True, vmem_limit_bytes=VMEM_LIMIT

time: 35 us -> 34.6 us (0.989)
  Pallas kernels: 33.9 us -> 33.5 us
    pallas_call x1, Pallas kernels: 33.9 us -> 33.5 us  [per_device(): pl.pallas_call(functools.partial(kernel, n_dom, n_sub), out_shape=pltpu.V...]
where the time goes in v3:
time: 34.6 us; the launch traced here: 34.1 us
  Pallas kernels  33.5 us (97%)
  local copies, waits for them, and re-layouts  0.64 us (2%)
    pallas_call x1, Pallas kernels, per_device(): pl.pallas_call(functools.partial(kernel, n_dom, n_sub), out_shape=pltpu.V...  33.5 us

profile of v3, /device:TPU:1, one launch (start us, length us, event | category | flops | bytes accessed | tf_op | source)
XLA Modules:
  0.0 34.1 jit_solution(2764664591800404427)
XLA Ops:
  0.0 33.5 %shard_map.109 = f32[9,16,56]{2,1,0:T(8,128)S(1)} custom-call(s32[16]{0:T(128)} %levels_hbm.1, s32[4,16]{1,0:T(4,128)} %source_hbm.1, s32[4]{0:T(128)} %send_hbm.1, f32[9,9]{1,0:T(8,128)} %fault_flux_hbm.1, s32[4,16]{1,0:T(4,128)} %fault_faces_hbm.1, f32[9,16,56]{2,1,0:T(8,128)} %bitcast.10, f32[3,56,56]{2,1,0:T(8,128)} %stiff_hbm.1, f32[21,4,56]{2,1,0:T(4,128)} %bitcast.11, ...), custom_call_target="tpu_custom_call" | custom-call | tf_op jit(solution)/shard_map/pallas_call | solution.py:435
  33.5 0.6 %copy.13 = f32[9,56,16]{1,2,0:T(8,128)} copy(f32[9,56,16]{1,2,0:T(8,128)S(1)} %bitcast.6) | data formatting | bytes 64512

commit v4 on v3

--- a/solution.py
+++ b/solution.py
@@ -16,6 +16,19 @@
 E = 16
 SLOTS = 12
 VMEM_LIMIT = 24 * 2**20
+FARTHEST_FIRST = (
+    (-1, 2),
+    (1, 2),
+    (-1, 1),
+    (1, 1),
+    (-1, 3),
+    (1, 3),
+    (0, 2),
+    (-1, 0),
+    (1, 0),
+    (0, 1),
+    (0, 3),
+)
 MESH = pl.DeviceIdType.MESH
 F32 = jnp.float32
 BF16 = jnp.bfloat16
@@ -149,6 +162,7 @@
     wv_ref,
     pw_ref,
     pt3_ref,
+    ptw_ref,
     cs_ref,
     cm_ref,
     cc_ref,
@@ -162,11 +176,8 @@
     dom = lax.axis_index("dom")
     sub = lax.axis_index("sub")
     peers = []
-    for delta in (-1, 1, 0):
-        for turn in (2, 1, 3, 0):
-            if delta == 0 and turn == 0:
-                continue
-            peers.append((delta, lax.rem(dom + delta + n_dom, n_dom), lax.rem(sub + turn, n_sub)))
+    for delta, turn in FARTHEST_FIRST:
+        peers.append((delta, lax.rem(dom + delta + n_dom, n_dom), lax.rem(sub + turn, n_sub)))
 
     barrier = pltpu.get_barrier_semaphore()
     for _, to_dom, to_sub in peers:
@@ -246,19 +257,25 @@
         return (coef_ref[v] * field).sum(axis=0)
 
     def with_star(weights_ref, left):
-        field = dot(left, weights_ref[...]).reshape(V, 8, 384)
+        return star_sum(dot(left, weights_ref[...]))
+
+    def star_sum(field):
+        field = field.reshape(V, 8, 384)
         result = []
         for v in range(V):
             total = contract(cs_ref, field, v)
             result.append(total[:, 0:128] + total[:, 128:256] + total[:, 256:384])
         return jnp.concatenate(result, axis=0)
 
-    def series(start, want_second):
+    def series(start, want_second, opening=None):
         current = start
         first = FIRST[0] * current
         second = SECOND[0] * current if want_second else None
         for k in range(1, ORDER):
-            current = with_star(wd_ref, lhs3(current))
+            if k == 1 and opening is not None:
+                current = star_sum(opening)
+            else:
+                current = with_star(wd_ref, lhs3(current))
             first = first + FIRST[k] * current
             if want_second:
                 second = second + SECOND[k] * current
@@ -345,8 +362,11 @@
         return dot(pick_local, jnp.concatenate([stack2(table[0]), stack2(table[1])], axis=1))
 
     def beside_faces(turn, near):
-        far = dot(pick_remote, stack2(recv_ref[turn].reshape(8 * SLOTS, 128)))
-        faces = from_table(near[:, 0:128] + far[0:64], near[:, 128:256] + far[64:128])
+        arrived = stack2(recv_ref[turn].reshape(8 * SLOTS, 128))
+        faces = from_table(
+            near[:, 0:128] + dot(pick_remote[0:64], arrived),
+            near[:, 128:256] + dot(pick_remote[64:128], arrived),
+        )
         return jnp.concatenate(faces, axis=0).reshape(V, 8, 256)
 
     left = lhs3(first_half)
@@ -386,17 +406,22 @@
             flux_ref[8 * v : 8 * v + 8, :] = contract(cm_ref, field, v)
         return volume
 
-    def far_side(base, turn, near):
+    def fluxes(turn, near):
         field = beside_faces(turn, near)
         total = jnp.concatenate([contract(cc_ref, field, v) for v in range(V)], axis=0)
-        return base - dot(lhs3(total + flux_ref[...]), pt3_ref[...])
+        hi, lo = split(total + flux_ref[...])
+        return jnp.concatenate([hi, lo], axis=1), hi
 
     near = local_part(table)
     base = dofs + own_side(left, faces)
+    base_slopes = dot(lhs3(base), wd_ref[...])
+    ptw_ref[...] = rhs3(dot(lhs3(pt), wd_ref[...]))
     finish_exchange(0, copies)
-    moved = far_side(base, 0, near)
-
-    again, _ = series(moved, False)
+    both, hi = fluxes(0, near)
+    opening = base_slopes - dot(both, ptw_ref[0:512, :]) - dot(hi, ptw_ref[512:768, :])
+    moved = base - dot(both, pt3_ref[0:512, :]) - dot(hi, pt3_ref[512:768, :])
+
+    again, _ = series(moved, False, opening)
     carried = jnp.where(fine, again, second_half)
     left = lhs3(carried)
     faces = dot(left, pw_ref[...])
@@ -409,7 +434,8 @@
     all_messages(0).wait_send()
     all_messages(1).wait_send()
     finish_exchange(1, copies)
-    after = far_side(base, 1, near)
+    both, hi = fluxes(1, near)
+    after = base - dot(both, pt3_ref[0:512, :]) - dot(hi, pt3_ref[512:768, :])
     for v in range(V):
         out_ref[v, 0:8, :] = after[8 * v : 8 * v + 8, 0:M]
         out_ref[v, 8:16, :] = after[8 * v : 8 * v + 8, 64 : 64 + M]
@@ -457,6 +483,7 @@
             pltpu.VMEM((384, 384), BF16),
             pltpu.VMEM((384, 256), BF16),
             pltpu.VMEM((768, 128), BF16),
+            pltpu.VMEM((768, 384), BF16),
             pltpu.VMEM((V, V, 8, 384), F32),
             pltpu.VMEM((V, V, 8, 256), F32),
             pltpu.VMEM((V, V, 8, 256), F32),

time: 34.6 us -> 34.4 us (level)
  no operation moved by 1% of the time
where the time goes in v4:
time: 34.4 us; the launch traced here: 34 us
  Pallas kernels  33.4 us (97%)
  local copies, waits for them, and re-layouts  0.64 us (2%)
    pallas_call x1, Pallas kernels, per_device(): pl.pallas_call(functools.partial(kernel, n_dom, n_sub), out_shape=pltpu.V...  33.4 us

profile of v4, /device:TPU:1, one launch (start us, length us, event | category | flops | bytes accessed | tf_op | source)
XLA Modules:
  0.0 34.0 jit_solution(8781487522860898430)
XLA Ops:
  0.0 33.4 %shard_map.109 = f32[9,16,56]{2,1,0:T(8,128)S(1)} custom-call(s32[16]{0:T(128)} %levels_hbm.1, s32[4,16]{1,0:T(4,128)} %source_hbm.1, s32[4]{0:T(128)} %send_hbm.1, f32[9,9]{1,0:T(8,128)} %fault_flux_hbm.1, s32[4,16]{1,0:T(4,128)} %fault_faces_hbm.1, f32[9,16,56]{2,1,0:T(8,128)} %bitcast.10, f32[3,56,56]{2,1,0:T(8,128)} %stiff_hbm.1, f32[21,4,56]{2,1,0:T(4,128)} %bitcast.11, ...), custom_call_target="tpu_custom_call" | custom-call | tf_op jit(solution)/shard_map/pallas_call | solution.py:461
  33.4 0.6 %copy.13 = f32[9,56,16]{1,2,0:T(8,128)} copy(f32[9,56,16]{1,2,0:T(8,128)S(1)} %bitcast.6) | data formatting | bytes 64512

commit v5 on v4

--- a/solution.py
+++ b/solution.py
@@ -172,6 +172,7 @@
     in_sem,
     send_sem,
     recv_sem,
+    across_sem,
 ):
     dom = lax.axis_index("dom")
     sub = lax.axis_index("sub")
@@ -179,9 +180,28 @@
     for delta, turn in FARTHEST_FIRST:
         peers.append((delta, lax.rem(dom + delta + n_dom, n_dom), lax.rem(sub + turn, n_sub)))
 
+    odd = lax.rem(dom, 2)
+    step = 2 * odd - 1
+    partner = dom - step
+    across = lax.rem(dom + step + n_dom, n_dom)
+    behind = lax.rem(dom + 2 * step + n_dom, n_dom)
+    subs = [lax.rem(sub + turn, n_sub) for turn in range(4)]
     barrier = pltpu.get_barrier_semaphore()
-    for _, to_dom, to_sub in peers:
-        pl.semaphore_signal(barrier, inc=1, device_id=(to_dom, to_sub), device_id_type=MESH)
+
+    def signal(to_dom, to_sub, which=barrier):
+        pl.semaphore_signal(which, inc=1, device_id=(to_dom, to_sub), device_id_type=MESH)
+
+    signal(behind, sub)
+    for turn in (2, 1, 3):
+        signal(dom, subs[turn])
+
+    @pl.when(odd == 0)
+    def _():
+        for turn in (2, 1, 3):
+            signal(behind, subs[turn])
+
+    for turn in (2, 1, 3, 0):
+        signal(partner, subs[turn])
 
     loads = [
         pltpu.make_async_copy(src, dst, in_sem.at[i])
@@ -326,37 +346,68 @@
 
     dofs = x_ref[...]
     first_half, second_half = series(dofs, True)
-
-    def start_exchange(turn, table):
+    pl.semaphore_wait(barrier, 11 - 3 * odd)
+    signal(partner, sub, across_sem)
+
+    def make_message(turn, table):
         stacked = jnp.concatenate([stack2(table[0]), stack2(table[1])], axis=0)
         message = dot(pick_send, stacked)
         msg_ref[turn] = message
         recv_ref[turn, 4 + sub] = message
-        return [
-            pltpu.make_async_remote_copy(
-                src_ref=msg_ref.at[turn],
-                dst_ref=recv_ref.at[turn, 4 * (1 - delta) + sub],
-                send_sem=send_sem.at[turn],
-                recv_sem=recv_sem.at[turn],
-                device_id=(to_dom, to_sub),
-                device_id_type=MESH,
-            )
-            for delta, to_dom, to_sub in peers
-        ]
-
-    def all_messages(turn):
-        some = recv_ref.at[turn, pl.ds(0, len(peers))]
+
+    def message_to(turn, slot, to_dom, to_sub, arrival):
+        return pltpu.make_async_remote_copy(
+            src_ref=msg_ref.at[turn],
+            dst_ref=recv_ref.at[turn, slot],
+            send_sem=send_sem.at[turn],
+            recv_sem=arrival,
+            device_id=(to_dom, to_sub),
+            device_id_type=MESH,
+        )
+
+    def several(turn, count, arrival):
+        some = recv_ref.at[turn, pl.ds(0, count)]
         return pltpu.make_async_remote_copy(
             src_ref=some,
             dst_ref=some,
             send_sem=send_sem.at[turn],
-            recv_sem=recv_sem.at[turn],
-            device_id=(dom, lax.rem(sub + 1, n_sub)),
+            recv_sem=arrival,
+            device_id=(dom, subs[1]),
             device_id_type=MESH,
         )
 
-    def finish_exchange(turn, copies):
-        all_messages(turn).wait_recv()
+    def start_first():
+        @pl.when(odd == 1)
+        def _():
+            pl.semaphore_wait(across_sem, 1)
+            for turn in (2, 1, 3, 0):
+                message_to(0, sub, across, subs[turn], recv_sem.at[0]).start()
+
+        for turn in (2, 1, 3):
+            message_to(0, 4 + sub, dom, subs[turn], recv_sem.at[2]).start()
+        for turn in (2, 1, 3, 0):
+            message_to(0, 8 * odd + sub, partner, subs[turn], recv_sem.at[0]).start()
+
+    def finish_first():
+        several(0, 3, recv_sem.at[2]).wait_recv()
+
+        @pl.when(odd == 0)
+        def _():
+            pl.semaphore_wait(across_sem, 1)
+            pltpu.make_async_remote_copy(
+                src_ref=recv_ref.at[0, pl.ds(4, 4)],
+                dst_ref=recv_ref.at[0, pl.ds(8, 4)],
+                send_sem=send_sem.at[0],
+                recv_sem=recv_sem.at[0],
+                device_id=(across, sub),
+                device_id_type=MESH,
+            ).start()
+
+        several(0, 8, recv_sem.at[0]).wait_recv()
+
+    def start_second():
+        for delta, to_dom, to_sub in peers:
+            message_to(1, 4 * (1 - delta) + sub, to_dom, to_sub, recv_sem.at[1]).start()
 
     def local_part(table):
         return dot(pick_local, jnp.concatenate([stack2(table[0]), stack2(table[1])], axis=1))
@@ -372,10 +423,8 @@
     left = lhs3(first_half)
     faces = dot(left, pw_ref[...])
     table = to_table(faces)
-    copies = start_exchange(0, table)
-    pl.semaphore_wait(barrier, len(peers))
-    for copy in copies:
-        copy.start()
+    make_message(0, table)
+    start_first()
 
     loads[4].wait()
     spread(
@@ -416,7 +465,7 @@
     base = dofs + own_side(left, faces)
     base_slopes = dot(lhs3(base), wd_ref[...])
     ptw_ref[...] = rhs3(dot(lhs3(pt), wd_ref[...]))
-    finish_exchange(0, copies)
+    finish_first()
     both, hi = fluxes(0, near)
     opening = base_slopes - dot(both, ptw_ref[0:512, :]) - dot(hi, ptw_ref[512:768, :])
     moved = base - dot(both, pt3_ref[0:512, :]) - dot(hi, pt3_ref[512:768, :])
@@ -426,14 +475,13 @@
     left = lhs3(carried)
     faces = dot(left, pw_ref[...])
     table = to_table(faces)
-    copies = start_exchange(1, table)
-    for copy in copies:
-        copy.start()
+    make_message(1, table)
+    start_second()
     near = local_part(table)
     base = moved + own_side(left, faces)
-    all_messages(0).wait_send()
-    all_messages(1).wait_send()
-    finish_exchange(1, copies)
+    for turn in range(2):
+        several(turn, len(peers), recv_sem.at[turn]).wait_send()
+    several(1, len(peers), recv_sem.at[1]).wait_recv()
     both, hi = fluxes(1, near)
     after = base - dot(both, pt3_ref[0:512, :]) - dot(hi, pt3_ref[512:768, :])
     for v in range(V):
@@ -492,7 +540,8 @@
             pltpu.VMEM((2, SLOTS, 8, 128), F32),
             pltpu.SemaphoreType.DMA((11,)),
             pltpu.SemaphoreType.DMA((2,)),
-            pltpu.SemaphoreType.DMA((2,)),
+            pltpu.SemaphoreType.DMA((3,)),
+            pltpu.SemaphoreType.REGULAR,
         ],
         compiler_params=pltpu.CompilerParams(
             collective_id=0, has_side_effects=True, vmem_limit_bytes=VMEM_LIMIT

time: 34.4 us -> 34.5 us (level)
  no operation moved by 1% of the time
where the time goes in v5:
time: 34.5 us; the launch traced here: 34.3 us
  Pallas kernels  33.7 us (98%)
  local copies, waits for them, and re-layouts  0.64 us (2%)
    pallas_call x1, Pallas kernels, per_device(): pl.pallas_call(functools.partial(kernel, n_dom, n_sub), out_shape=pltpu.V...  33.7 us

profile of v5, /device:TPU:1, one launch (start us, length us, event | category | flops | bytes accessed | tf_op | source)
XLA Modules:
  0.0 34.3 jit_solution(3205089809293318636)
XLA Ops:
  0.0 33.7 %shard_map.109 = f32[9,16,56]{2,1,0:T(8,128)S(1)} custom-call(s32[16]{0:T(128)} %levels_hbm.1, s32[4,16]{1,0:T(4,128)} %source_hbm.1, s32[4]{0:T(128)} %send_hbm.1, f32[9,9]{1,0:T(8,128)} %fault_flux_hbm.1, s32[4,16]{1,0:T(4,128)} %fault_faces_hbm.1, f32[9,16,56]{2,1,0:T(8,128)} %bitcast.10, f32[3,56,56]{2,1,0:T(8,128)} %stiff_hbm.1, f32[21,4,56]{2,1,0:T(4,128)} %bitcast.11, ...), custom_call_target="tpu_custom_call" | custom-call | tf_op jit(solution)/shard_map/pallas_call | solution.py:509
  33.7 0.6 %copy.13 = f32[9,56,16]{1,2,0:T(8,128)} copy(f32[9,56,16]{1,2,0:T(8,128)S(1)} %bitcast.6) | data formatting | bytes 64512

commit v6 on v5

--- a/solution.py
+++ b/solution.py
@@ -180,6 +180,42 @@
     for delta, turn in FARTHEST_FIRST:
         peers.append((delta, lax.rem(dom + delta + n_dom, n_dom), lax.rem(sub + turn, n_sub)))
 
+    def strided(src, dst, count, at):
+        return [
+            pltpu.make_async_copy(
+                src.at[:, w], dst.at[:, pl.ds(4 * w, count), :], in_sem.at[at]
+            )
+            for w in range(V)
+        ]
+
+    star_loads = strided(star_hbm, star_ref, 3, 8)
+    minus_loads = strided(minus_hbm, minus_ref, 4, 9)
+    plus_loads = strided(plus_hbm, plus_ref, 4, 10)
+    loads = [
+        pltpu.make_async_copy(src, dst, in_sem.at[i])
+        for i, (src, dst) in enumerate(
+            (
+                (stiff_hbm, stiff_ref),
+                (dofs_hbm, dofs_ref),
+                (proj_hbm, proj_ref),
+                (send_hbm, send_ref),
+                (levels_hbm, levels_ref),
+                (source_hbm, source_ref),
+                (fault_flux_hbm, fault_flux_ref),
+                (fault_faces_hbm, fault_faces_ref),
+            )
+        )
+    ]
+    for load in loads[0:1] + star_loads + loads[1:] + minus_loads + plus_loads:
+        load.start()
+
+    def wait_whole(src, at):
+        pltpu.make_async_copy(src, src, in_sem.at[at]).wait()
+
+    def wait(*which):
+        for load in which:
+            load.wait()
+
     odd = lax.rem(dom, 2)
     step = 2 * odd - 1
     partner = dom - step
@@ -203,33 +239,12 @@
     for turn in (2, 1, 3, 0):
         signal(partner, subs[turn])
 
-    loads = [
-        pltpu.make_async_copy(src, dst, in_sem.at[i])
-        for i, (src, dst) in enumerate(
-            (
-                (stiff_hbm, stiff_ref),
-                (star_hbm, star_ref),
-                (dofs_hbm, dofs_ref),
-                (proj_hbm, proj_ref),
-                (minus_hbm, minus_ref),
-                (plus_hbm, plus_ref),
-                (levels_hbm, levels_ref),
-                (source_hbm, source_ref),
-                (send_hbm, send_ref),
-                (fault_flux_hbm, fault_flux_ref),
-                (fault_faces_hbm, fault_faces_ref),
-            )
-        )
-    ]
-    for load in loads:
-        load.start()
-
     block_ref[...] = jnp.zeros(block_ref.shape, F32)
     pt_ref[...] = jnp.zeros(pt_ref.shape, F32)
     x_ref[...] = jnp.zeros(x_ref.shape, F32)
     row_ref[...] = jnp.zeros(row_ref.shape, F32)
 
-    loads[0].wait()
+    wait(loads[0])
     for d in range(3):
         block_ref[d, 0:M, 0:M] = stiff_ref[d]
         block_ref[d, 64 : 64 + M, 64 : 64 + M] = stiff_ref[d]
@@ -237,6 +252,22 @@
         block = block_ref[d]
         wd_ref[:, 128 * d : 128 * d + 128] = rhs3(block.T)
         wv_ref[:, 128 * d : 128 * d + 128] = rhs3(block)
+
+    wait(loads[2])
+    for f in range(4):
+        for half in range(2):
+            at = 64 * f + 32 * half
+            pt_ref[at : at + J, 64 * half : 64 * half + M] = proj_ref[:, f, :]
+    pt = pt_ref[...]
+    pw_ref[...] = rhs3(pt.T)
+
+    wait(loads[3])
+    row = rows((8, 256))
+    lane = lanes((8, 256))
+    wanted = jnp.full((8, 256), -1, jnp.int32)
+    for s in range(4):
+        wanted = jnp.where(row % 4 == s, send_ref[s], wanted)
+    pick_send = ((lane % 64 == wanted) & (lane // 128 == row // 4)).astype(F32).astype(BF16)
 
     def spread(make_row, groups, part_width, fill, coef_ref):
         width = 128 * coef_ref.shape[3] // 128
@@ -259,16 +290,16 @@
             ).astype(BF16)
             coef_ref[v] = dot(left, repeat).reshape(V, 8, width)
 
-    loads[1].wait()
+    wait_whole(star_hbm, 8)
     spread(
-        lambda v: jnp.concatenate([star_ref[v, :, d, :] for d in range(3)], axis=1),
+        lambda v: jnp.concatenate([star_ref[v, pl.ds(d, V, stride=4), :] for d in range(3)], axis=1),
         3,
         64,
         M,
         cs_ref,
     )
 
-    loads[2].wait()
+    wait(loads[1])
     for v in range(V):
         x_ref[8 * v : 8 * v + 8, 0:M] = dofs_ref[v, 0:8, :]
         x_ref[8 * v : 8 * v + 8, 64 : 64 + M] = dofs_ref[v, 8:16, :]
@@ -301,24 +332,90 @@
                 second = second + SECOND[k] * current
         return first, second
 
-    loads[3].wait()
-    for f in range(4):
-        for half in range(2):
-            at = 64 * f + 32 * half
-            pt_ref[at : at + J, 64 * half : 64 * half + M] = proj_ref[:, f, :]
-    pt = pt_ref[...]
-    pw_ref[...] = rhs3(pt.T)
+    dofs = x_ref[...]
+    first_half, second_half = series(dofs, True)
+    pl.semaphore_wait(barrier, 11 - 3 * odd)
+    signal(partner, sub, across_sem)
+
+    def make_message(turn, table):
+        stacked = jnp.concatenate([stack2(table[0]), stack2(table[1])], axis=0)
+        message = dot(pick_send, stacked)
+        msg_ref[turn] = message
+        recv_ref[turn, 4 + sub] = message
+
+    def message_to(turn, slot, to_dom, to_sub, arrival):
+        return pltpu.make_async_remote_copy(
+            src_ref=msg_ref.at[turn],
+            dst_ref=recv_ref.at[turn, slot],
+            send_sem=send_sem.at[turn],
+            recv_sem=arrival,
+            device_id=(to_dom, to_sub),
+            device_id_type=MESH,
+        )
+
+    def several(turn, count, arrival):
+        some = recv_ref.at[turn, pl.ds(0, count)]
+        return pltpu.make_async_remote_copy(
+            src_ref=some,
+            dst_ref=some,
+            send_sem=send_sem.at[turn],
+            recv_sem=arrival,
+            device_id=(dom, subs[1]),
+            device_id_type=MESH,
+        )
+
+    def start_first():
+        @pl.when(odd == 1)
+        def _():
+            pl.semaphore_wait(across_sem, 1)
+            for turn in (2, 1, 3, 0):
+                message_to(0, sub, across, subs[turn], recv_sem.at[0]).start()
+
+        for turn in (2, 1, 3):
+            message_to(0, 4 + sub, dom, subs[turn], recv_sem.at[2]).start()
+        for turn in (2, 1, 3, 0):
+            message_to(0, 8 * odd + sub, partner, subs[turn], recv_sem.at[0]).start()
+
+    def finish_first():
+        several(0, 3, recv_sem.at[2]).wait_recv()
+
+        @pl.when(odd == 0)
+        def _():
+            pl.semaphore_wait(across_sem, 1)
+            pltpu.make_async_remote_copy(
+                src_ref=recv_ref.at[0, pl.ds(4, 4)],
+                dst_ref=recv_ref.at[0, pl.ds(8, 4)],
+                send_sem=send_sem.at[0],
+                recv_sem=recv_sem.at[0],
+                device_id=(across, sub),
+                device_id_type=MESH,
+            ).start()
+
+        several(0, 8, recv_sem.at[0]).wait_recv()
+
+    def start_second():
+        for delta, to_dom, to_sub in peers:
+            message_to(1, 4 * (1 - delta) + sub, to_dom, to_sub, recv_sem.at[1]).start()
+
+    def local_part(table):
+        return dot(pick_local, jnp.concatenate([stack2(table[0]), stack2(table[1])], axis=1))
+
+    def beside_faces(turn, near):
+        arrived = stack2(recv_ref[turn].reshape(8 * SLOTS, 128))
+        faces = from_table(
+            near[:, 0:128] + dot(pick_remote[0:64], arrived),
+            near[:, 128:256] + dot(pick_remote[64:128], arrived),
+        )
+        return jnp.concatenate(faces, axis=0).reshape(V, 8, 256)
+
+    left = lhs3(first_half)
+    faces = dot(left, pw_ref[...])
+    table = to_table(faces)
+    make_message(0, table)
+    start_first()
+
     pt3_ref[...] = rhs3(pt)
-
-    for i in (6, 7, 8):
-        loads[i].wait()
-    row = rows((8, 256))
-    lane = lanes((8, 256))
-    wanted = jnp.full((8, 256), -1, jnp.int32)
-    for s in range(4):
-        wanted = jnp.where(row % 4 == s, send_ref[s], wanted)
-    pick_send = ((lane % 64 == wanted) & (lane // 128 == row // 4)).astype(F32).astype(BF16)
-
+    wait(*loads[4:6])
     local_rows, remote_rows = [], []
     row = rows()
     lane = lanes()
@@ -344,102 +441,20 @@
         fine = jnp.where(here & (levels_ref[e] == 0), 1, fine)
     fine = jnp.concatenate([fine] * V, axis=0) == 1
 
-    dofs = x_ref[...]
-    first_half, second_half = series(dofs, True)
-    pl.semaphore_wait(barrier, 11 - 3 * odd)
-    signal(partner, sub, across_sem)
-
-    def make_message(turn, table):
-        stacked = jnp.concatenate([stack2(table[0]), stack2(table[1])], axis=0)
-        message = dot(pick_send, stacked)
-        msg_ref[turn] = message
-        recv_ref[turn, 4 + sub] = message
-
-    def message_to(turn, slot, to_dom, to_sub, arrival):
-        return pltpu.make_async_remote_copy(
-            src_ref=msg_ref.at[turn],
-            dst_ref=recv_ref.at[turn, slot],
-            send_sem=send_sem.at[turn],
-            recv_sem=arrival,
-            device_id=(to_dom, to_sub),
-            device_id_type=MESH,
-        )
-
-    def several(turn, count, arrival):
-        some = recv_ref.at[turn, pl.ds(0, count)]
-        return pltpu.make_async_remote_copy(
-            src_ref=some,
-            dst_ref=some,
-            send_sem=send_sem.at[turn],
-            recv_sem=arrival,
-            device_id=(dom, subs[1]),
-            device_id_type=MESH,
-        )
-
-    def start_first():
-        @pl.when(odd == 1)
-        def _():
-            pl.semaphore_wait(across_sem, 1)
-            for turn in (2, 1, 3, 0):
-                message_to(0, sub, across, subs[turn], recv_sem.at[0]).start()
-
-        for turn in (2, 1, 3):
-            message_to(0, 4 + sub, dom, subs[turn], recv_sem.at[2]).start()
-        for turn in (2, 1, 3, 0):
-            message_to(0, 8 * odd + sub, partner, subs[turn], recv_sem.at[0]).start()
-
-    def finish_first():
-        several(0, 3, recv_sem.at[2]).wait_recv()
-
-        @pl.when(odd == 0)
-        def _():
-            pl.semaphore_wait(across_sem, 1)
-            pltpu.make_async_remote_copy(
-                src_ref=recv_ref.at[0, pl.ds(4, 4)],
-                dst_ref=recv_ref.at[0, pl.ds(8, 4)],
-                send_sem=send_sem.at[0],
-                recv_sem=recv_sem.at[0],
-                device_id=(across, sub),
-                device_id_type=MESH,
-            ).start()
-
-        several(0, 8, recv_sem.at[0]).wait_recv()
-
-    def start_second():
-        for delta, to_dom, to_sub in peers:
-            message_to(1, 4 * (1 - delta) + sub, to_dom, to_sub, recv_sem.at[1]).start()
-
-    def local_part(table):
-        return dot(pick_local, jnp.concatenate([stack2(table[0]), stack2(table[1])], axis=1))
-
-    def beside_faces(turn, near):
-        arrived = stack2(recv_ref[turn].reshape(8 * SLOTS, 128))
-        faces = from_table(
-            near[:, 0:128] + dot(pick_remote[0:64], arrived),
-            near[:, 128:256] + dot(pick_remote[64:128], arrived),
-        )
-        return jnp.concatenate(faces, axis=0).reshape(V, 8, 256)
-
-    left = lhs3(first_half)
-    faces = dot(left, pw_ref[...])
-    table = to_table(faces)
-    make_message(0, table)
-    start_first()
-
-    loads[4].wait()
+    wait_whole(minus_hbm, 9)
     spread(
-        lambda v: jnp.concatenate([minus_ref[v, :, f, :] for f in range(4)], axis=1),
+        lambda v: jnp.concatenate([minus_ref[v, pl.ds(f, V, stride=4), :] for f in range(4)], axis=1),
         4,
         32,
         J,
         cm_ref,
     )
-    for i in (5, 9, 10):
-        loads[i].wait()
+    wait_whole(plus_hbm, 10)
+    wait(*loads[6:8])
     on_fault = jnp.concatenate([fault_faces_ref[f : f + 1, :] for f in range(4)], axis=1) == 1
 
     def coupling_row(v):
-        plus = jnp.concatenate([plus_ref[v, :, f, :] for f in range(4)], axis=1)
+        plus = jnp.concatenate([plus_ref[v, pl.ds(f, V, stride=4), :] for f in range(4)], axis=1)
         w_at = rows((V, 4 * E))
         friction = jnp.zeros((V, 4 * E), F32)
         for w in range(V):
@@ -520,9 +535,9 @@
             pltpu.VMEM((V, E, M), F32),
             pltpu.VMEM((3, M, M), F32),
             pltpu.VMEM((J, 4, M), F32),
-            pltpu.VMEM((V, V, 3, E), F32),
-            pltpu.VMEM((V, V, 4, E), F32),
-            pltpu.VMEM((V, V, 4, E), F32),
+            pltpu.VMEM((V, 4 * V, E), F32),
+            pltpu.VMEM((V, 4 * V, E), F32),
+            pltpu.VMEM((V, 4 * V, E), F32),
             pltpu.VMEM((3, 128, 128), F32),
             pltpu.VMEM((256, 128), F32),
             pltpu.VMEM((72, 128), F32),

time: 34.5 us -> 34.3 us (level)
  no operation moved by 1% of the time
where the time goes in v6:
time: 34.3 us; the launch traced here: 34.1 us
  Pallas kernels  33.5 us (98%)
  local copies, waits for them, and re-layouts  0.64 us (2%)
    pallas_call x1, Pallas kernels, per_device(): pl.pallas_call(functools.partial(kernel, n_dom, n_sub), out_shape=pltpu.V...  33.5 us

profile of v6, /device:TPU:1, one launch (start us, length us, event | category | flops | bytes accessed | tf_op | source)
XLA Modules:
  0.0 34.1 jit_solution(259553493158870604)
XLA Ops:
  0.0 33.5 %shard_map.109 = f32[9,16,56]{2,1,0:T(8,128)S(1)} custom-call(s32[16]{0:T(128)} %levels_hbm.1, s32[4,16]{1,0:T(4,128)} %source_hbm.1, s32[4]{0:T(128)} %send_hbm.1, f32[9,9]{1,0:T(8,128)} %fault_flux_hbm.1, s32[4,16]{1,0:T(4,128)} %fault_faces_hbm.1, f32[9,16,56]{2,1,0:T(8,128)} %bitcast.10, f32[3,56,56]{2,1,0:T(8,128)} %stiff_hbm.1, f32[21,4,56]{2,1,0:T(4,128)} %bitcast.11, ...), custom_call_target="tpu_custom_call" | custom-call | tf_op jit(solution)/shard_map/pallas_call | solution.py:524
  33.5 0.6 %copy.13 = f32[9,56,16]{1,2,0:T(8,128)} copy(f32[9,56,16]{1,2,0:T(8,128)S(1)} %bitcast.6) | data formatting | bytes 64512

commit v7 on v6

--- a/solution.py
+++ b/solution.py
@@ -397,6 +397,9 @@
         for delta, to_dom, to_sub in peers:
             message_to(1, 4 * (1 - delta) + sub, to_dom, to_sub, recv_sem.at[1]).start()
 
+    def face_values(left):
+        return dot(left[:, 0:256], pw_ref[0:256, :]) + dot(left[:, 256:384], pw_ref[256:384, :])
+
     def local_part(table):
         return dot(pick_local, jnp.concatenate([stack2(table[0]), stack2(table[1])], axis=1))
 
@@ -409,7 +412,7 @@
         return jnp.concatenate(faces, axis=0).reshape(V, 8, 256)
 
     left = lhs3(first_half)
-    faces = dot(left, pw_ref[...])
+    faces = face_values(left)
     table = to_table(faces)
     make_message(0, table)
     start_first()
@@ -488,7 +491,7 @@
     again, _ = series(moved, False, opening)
     carried = jnp.where(fine, again, second_half)
     left = lhs3(carried)
-    faces = dot(left, pw_ref[...])
+    faces = face_values(left)
     table = to_table(faces)
     make_message(1, table)
     start_second()

time: 34.3 us -> 34.3 us (level)
  no operation moved by 1% of the time
where the time goes in v7:
time: 34.3 us; the launch traced here: 34.1 us
  Pallas kernels  33.5 us (98%)
  local copies, waits for them, and re-layouts  0.64 us (2%)
    pallas_call x1, Pallas kernels, per_device(): pl.pallas_call(functools.partial(kernel, n_dom, n_sub), out_shape=pltpu.V...  33.5 us

profile of v7, /device:TPU:1, one launch (start us, length us, event | category | flops | bytes accessed | tf_op | source)
XLA Modules:
  0.0 34.1 jit_solution(11368761246076852485)
XLA Ops:
  0.0 33.5 %shard_map.109 = f32[9,16,56]{2,1,0:T(8,128)S(1)} custom-call(s32[16]{0:T(128)} %levels_hbm.1, s32[4,16]{1,0:T(4,128)} %source_hbm.1, s32[4]{0:T(128)} %send_hbm.1, f32[9,9]{1,0:T(8,128)} %fault_flux_hbm.1, s32[4,16]{1,0:T(4,128)} %fault_faces_hbm.1, f32[9,16,56]{2,1,0:T(8,128)} %bitcast.10, f32[3,56,56]{2,1,0:T(8,128)} %stiff_hbm.1, f32[21,4,56]{2,1,0:T(4,128)} %bitcast.11, ...), custom_call_target="tpu_custom_call" | custom-call | tf_op jit(solution)/shard_map/pallas_call | solution.py:527
  33.5 0.6 %copy.13 = f32[9,56,16]{1,2,0:T(8,128)} copy(f32[9,56,16]{1,2,0:T(8,128)S(1)} %bitcast.6) | data formatting | bytes 64512
